TPU v7x, 256 devices: a whole 4x4x8 slice. The times are simulated.
256 devices in a mesh: wide: 16 (over z, y_hi), narrow: 8 (over x, y_lo), grp: 2 (over core).
Axes of the slice: x: 4, y: 4 (y_hi: 2, y_lo: 2; y = y_hi * 2 + y_lo), z: 8, core: 2. Of those that a mesh axis runs over, the one named last changes fastest.
Arguments:
- boundary_block: float32 [16, 1024, 16384], P(None, ('narrow', 'grp'), 'wide'), may hold values from -4 to 4
- schur_blocks: float32 [8, 1536, 1536], P('narrow', ('wide', 'grp')), may hold values from -2 to 2
- interface_rows: int32 [8, 1536], P('narrow'), may hold values from 0 to 2047, as said below
- live_rows: int32 [8], P('narrow'), may hold values from 1 to 1536, 9216 in all
- row_scale: float32 [16, 1024], P('wide', ('narrow', 'grp')), may hold values from 0.4 to 1.2
- excitation: float32 [16, 1024, 128], P('wide', ('narrow', 'grp')), may hold values from -6 to 6
Outputs:
- traces: float32 [16, 1024, 128], P('wide', ('narrow', 'grp'))
- residual: float32 [16, 1024, 128], P('wide', ('narrow', 'grp'))
Inputs may be any that keep to these rules, and one draw needn't show every extreme that they name: `interface_rows`: each substructure's row holds 1536 different positions, 0 to 2047; within each aligned block of 48 slots, at most 2 positions lie in one aligned range of 64 positions, and every substructure reaches 2 in some block.
All inputs are finite; a program needn't handle non-finite values. No bound on the sum of `live_rows` on one device may be relied on, other than what follows from the above.
Results may differ from a plain program's by a relative error of at most 0.00016.
Values sent between devices are 32-bit elements; how exact they have to be, the bound alone decides.
A program may use at most 64 MiB of HBM per device.

v0:
```python
import jax
import jax.numpy as jnp
from jax import lax
from jax.sharding import PartitionSpec as P

ITERS = 3


RELAX = 0.35


def laid_out(tiles, dim):
    lengths = list(tiles.shape[1:])
    lengths[dim] *= tiles.shape[0]
    return jnp.moveaxis(tiles, 0, dim).reshape(lengths)


def from_everyone(value, axis):
    copies = jnp.broadcast_to(value, (lax.axis_size(axis), *value.shape))
    return lax.all_to_all(copies, axis, split_axis=0, concat_axis=0, tiled=True)


def gather_directly(value, axis, dim):
    return laid_out(from_everyone(value, axis), dim)


def cut_along(value, dim, devices):
    lengths = value.shape
    tiles = value.reshape(*lengths[:dim], devices, lengths[dim] // devices, *lengths[dim + 1 :])
    return jnp.moveaxis(tiles, dim, 0)


def summed_on_arrival(value, axis, dim):
    devices = lax.axis_size(axis)
    tiles = lax.all_to_all(cut_along(value, dim, devices), axis, 0, 0, tiled=True)
    return jnp.sum(tiles, axis=0)


def slot_ranks(owners):
    count = owners.shape[-1]
    same = owners[..., :, None] == owners[..., None, :]
    earlier = jnp.arange(count)[None, :] < jnp.arange(count)[:, None]
    return jnp.sum((same & earlier).astype(jnp.int32), axis=-1)


def on_device(boundary_block, schur_blocks, interface_rows, live_rows, row_scale, excitation):
    piece_rows = excitation.shape[1]
    wide_size = lax.axis_size("wide")
    grp_size = lax.axis_size("grp")
    blocks = wide_size * grp_size
    panel_size = blocks * piece_rows
    tile_block = boundary_block.reshape(-1, boundary_block.shape[2])
    row_weight = row_scale.reshape(piece_rows, 1)
    forcing = excitation[0]
    iface_size = interface_rows.shape[1]
    share_rows = schur_blocks.shape[1]
    sub_count = interface_rows.shape[0]
    row_group = lax.axis_index("wide") * grp_size + lax.axis_index("grp")
    positions = jnp.arange(iface_size, dtype=jnp.int32)
    live_mask = (positions[None, :] < live_rows[:, None]).astype(jnp.float32)
    own_rows = lax.dynamic_slice_in_dim(interface_rows, row_group * share_rows, share_rows, 1)
    slot_cap = (piece_rows + blocks - 1) // blocks
    targets = jnp.arange(blocks, dtype=jnp.int32)
    levels = jnp.arange(slot_cap, dtype=jnp.int32)
    send_owner = own_rows // piece_rows
    send_rank = slot_ranks(send_owner)
    send_pick = (
        (send_owner[:, None, None, :] == targets[None, :, None, None])
        & (send_rank[:, None, None, :] == levels[None, None, :, None])
    ).astype(jnp.float32)
    outgoing = jnp.einsum(
        "kots,ksm->oktm", send_pick, schur_blocks, precision=lax.Precision.HIGHEST
    )
    received = lax.all_to_all(outgoing, ("wide", "grp"), split_axis=0, concat_axis=0, tiled=True)
    block_rows = interface_rows.reshape(sub_count, blocks, share_rows)
    block_live = live_mask.reshape(sub_count, blocks, share_rows)
    block_owner = block_rows // piece_rows
    block_rank = slot_ranks(block_owner)
    take_pick = (
        (block_owner[:, :, None, :] == row_group)
        & (block_rank[:, :, None, :] == levels[None, None, :, None])
    ).astype(jnp.float32) * block_live[:, :, None, :]
    local_index = jnp.arange(piece_rows, dtype=jnp.int32)
    landing = ((block_rows % piece_rows)[..., None] == local_index).astype(jnp.float32)
    placement = jnp.einsum("kjts,kjsi->kjti", take_pick, landing, precision=lax.Precision.HIGHEST)
    traces = RELAX * row_weight * forcing
    residual = forcing
    for sweep in range(ITERS):
        wide_panel = gather_directly(traces[None], "wide", 0)
        full_panel = gather_directly(wide_panel[:, None], "grp", 1)
        stacked = wide_panel.reshape(-1, wide_panel.shape[-1])
        boundary = summed_on_arrival(
            lax.dot_general(
                tile_block,
                stacked,
                (((0,), (0,)), ((), ())),
                precision=lax.Precision.HIGHEST,
                preferred_element_type=jnp.float32,
            ),
            ("narrow", "grp"),
            0,
        )
        flat_panel = full_panel.reshape(panel_size, -1)
        local_traces = jnp.take(flat_panel, interface_rows, axis=0) * live_mask[:, :, None]
        values = jnp.einsum(
            "jktm,kmr->kjtr", received, local_traces, precision=lax.Precision.HIGHEST
        )
        interface = jnp.einsum("kjti,kjtr->ir", placement, values, precision=lax.Precision.HIGHEST)
        residual = forcing - (boundary + interface)
        traces = traces + RELAX * row_weight * residual
    return (traces[None], residual[None])


def solution(mesh):
    placed = (
        P(None, ("narrow", "grp"), "wide"),
        P("narrow", ("wide", "grp"), None),
        P("narrow", None),
        P("narrow"),
        P("wide", ("narrow", "grp")),
        P("wide", ("narrow", "grp"), None),
    )
    return jax.shard_map(
        on_device,
        mesh=mesh,
        in_specs=placed,
        out_specs=(P("wide", ("narrow", "grp"), None), P("wide", ("narrow", "grp"), None)),
        check_vma=False,
    )
```

profile of v0, /device:TPU:1, one launch (start us, length us, event | category | flops | bytes accessed | tf_op | source)
XLA Modules:
  0.0 168.3 jit_solution(653237365371124477)
XLA Ops:
  0.6 0.0 copy-start
  0.6 0.7 multiply_bitcast_fusion
  1.3 0.8 bitcast_multiply_fusion
  2.2 0.8 broadcast_in_dim.22
  3.0 11.7 %all-to-all-start = ((f32[16,1,64,128]{3,2,1,0:T(8,128)}), f32[16,1,64,128]{3,2,1,0:T(8,128)S(1)}, u32[]{:S(2)}, u32[]{:S(2)}) async-start(f32[16,1,64,128]{3,2,1,0:T(8,128)} %broadcast_in_dim.22), calls=%async_computation | async-start | bytes 1048576 | tf_op jit(solution)/shard_map/all_to_all | solution.py:20
  15.4 0.8 fusion.56
  16.2 0.2 convert_reduce_fusion.1
  16.4 0.7 fusion.62
  17.1 0.1 reshape.472
  17.2 0.0 copy-done
  17.2 0.3 convolution_bitcast_fusion
  17.5 1.1 copy.29
  18.6 0.7 and_reduce_fusion
  19.4 12.6 %all-to-all-done = f32[16,1,64,128]{3,2,1,0:T(8,128)S(1)} async-done(((f32[16,1,64,128]{3,2,1,0:T(8,128)}), f32[16,1,64,128]{3,2,1,0:T(8,128)S(1)}, u32[]{:S(2)}, u32[]{:S(2)}) %all-to-all-start) | async-done | bytes 524320 | tf_op jit(solution)/shard_map/all_to_all | solution.py:20
  32.0 6.1 %all-to-all-start.2 = ((f32[32,1,2,1536]{3,2,1,0:T(2,128)}), f32[32,1,2,1536]{3,2,1,0:T(2,128)S(1)}, u32[]{:S(2)}, u32[]{:S(2)}) async-start(f32[32,1,2,1536]{3,2,1,0:T(2,128)} %copy.29), calls=%async_computation.2 | async-start | bytes 786432 | tf_op jit(solution)/shard_map/all_to_all | solution.py:74
  38.1 0.8 convert_reduce_fusion
  39.0 4.6 %convolution_bitcast_fusion.3 = f32[1024,128]{0,1:T(8,128)S(1)} fusion(f32[1024,128]{1,0:T(8,128)S(1)} %bitcast.130, f32[1024,1024]{1,0:T(8,128)} %bitcast.127), kind=kOutput, calls=%fused_computation.6 | convolution fusion | flops 1610612736 | bytes 5242880 | tf_op jit(solution)/shard_map/dot_general | solution.py:93
  43.6 1.0 copy.28
  44.5 7.8 %all-to-all-done.2 = f32[32,1,2,1536]{3,2,1,0:T(2,128)S(1)} async-done(((f32[32,1,2,1536]{3,2,1,0:T(2,128)}), f32[32,1,2,1536]{3,2,1,0:T(2,128)S(1)}, u32[]{:S(2)}, u32[]{:S(2)}) %all-to-all-start.2) | async-done | bytes 393248 | tf_op jit(solution)/shard_map/all_to_all | solution.py:74
  52.3 0.1 broadcast_in_dim.23
  52.4 5.7 %all_to_all.59 = f32[2,16,1,64,128]{4,3,1,2,0:T(8,128)S(1)} all-to-all(f32[2,16,1,64,128]{4,3,1,2,0:T(8,128)S(1)} %broadcast_in_dim.23), channel_id=1, replica_groups=mesh['wide'=16,'narrow'=8,'grp'=2] {'grp'}, dimensions={0} | all-to-all | bytes 2097152 | tf_op jit(solution)/shard_map/all_to_all | solution.py:20
  58.2 4.8 %all-to-all-start.1 = ((f32[16,64,128]{2,1,0:T(8,128)}), f32[16,64,128]{2,1,0:T(8,128)S(1)}, u32[]{:S(2)}, u32[]{:S(2)}) async-start(f32[16,64,128]{2,1,0:T(8,128)} %bitcast.5), calls=%async_computation.1 | async-start | bytes 1048576 | tf_op jit(solution)/shard_map/all_to_all | solution.py:35
  63.0 0.6 fusion.22
  63.5 0.1 copy.31
  63.7 0.0 copy-start.1
  63.7 2.6 %gather_fusion = f32[1536,128]{1,0:T(8,128)S(1)} fusion(f32[2048,128]{1,0:T(8,128)S(1)} %bitcast.125, s32[2048]{0:T(1024)S(1)} %pad_clamp_fusion), kind=kCustom, calls=%fused_computation.clone | custom fusion | bytes 1579008 | tf_op jit(solution)/shard_map/jit(_take)/gather | solution.py:104
  66.3 0.9 fusion.18
  67.2 5.5 %all-to-all-done.1 = f32[16,64,128]{2,1,0:T(8,128)S(1)} async-done(((f32[16,64,128]{2,1,0:T(8,128)}), f32[16,64,128]{2,1,0:T(8,128)S(1)}, u32[]{:S(2)}, u32[]{:S(2)}) %all-to-all-start.1) | async-done | bytes 524320 | tf_op jit(solution)/shard_map/all_to_all | solution.py:35
  72.7 0.0 copy-done.1
  72.7 0.2 fusion.3
  73.0 21.2 %all_to_all.60 = f32[16,1,64,128]{3,2,1,0:T(8,128)S(1)} all-to-all(f32[16,1,64,128]{3,2,1,0:T(8,128)S(1)} %broadcast_in_dim.24), channel_id=1, replica_groups=mesh['wide'=16,'narrow'=8,'grp'=2] {'wide'}, dimensions={0} | all-to-all | bytes 1048576 | tf_op jit(solution)/shard_map/all_to_all | solution.py:20
  94.2 4.6 %convolution_bitcast_fusion.2 = f32[1024,128]{0,1:T(8,128)S(1)} fusion(f32[1024,128]{1,0:T(8,128)S(1)} %bitcast.132, f32[1024,1024]{1,0:T(8,128)} %bitcast.128), kind=kOutput, calls=%fused_computation.5 | convolution fusion | flops 1610612736 | bytes 5242880 | tf_op jit(solution)/shard_map/dot_general | solution.py:93
  98.8 1.0 copy.33
  99.8 0.1 broadcast_in_dim.25
  99.9 7.0 %all_to_all.61 = f32[2,16,1,64,128]{4,3,1,2,0:T(8,128)S(1)} all-to-all(f32[2,16,1,64,128]{4,3,1,2,0:T(8,128)S(1)} %broadcast_in_dim.25), channel_id=1, replica_groups=mesh['wide'=16,'narrow'=8,'grp'=2] {'grp'}, dimensions={0} | all-to-all | bytes 2097152 | tf_op jit(solution)/shard_map/all_to_all | solution.py:20
  106.9 3.8 %all-to-all-start.5 = ((f32[16,64,128]{2,1,0:T(8,128)}), f32[16,64,128]{2,1,0:T(8,128)S(1)}, u32[]{:S(2)}, u32[]{:S(2)}) async-start(f32[16,64,128]{2,1,0:T(8,128)} %bitcast.23), calls=%async_computation.5 | async-start | bytes 1048576 | tf_op jit(solution)/shard_map/all_to_all | solution.py:35
  110.7 0.1 copy.34
  110.8 2.6 %gather_fusion.1 = f32[1536,128]{1,0:T(8,128)S(1)} fusion(f32[2048,128]{1,0:T(8,128)S(1)} %bitcast.126, s32[2048]{0:T(1024)S(1)} %pad_clamp_fusion), kind=kCustom, calls=%fused_computation.1.clone | custom fusion | bytes 1579008 | tf_op jit(solution)/shard_map/jit(_take)/gather | solution.py:104
  113.4 0.9 fusion.14
  114.3 6.1 %all-to-all-done.5 = f32[16,64,128]{2,1,0:T(8,128)S(1)} async-done(((f32[16,64,128]{2,1,0:T(8,128)}), f32[16,64,128]{2,1,0:T(8,128)S(1)}, u32[]{:S(2)}, u32[]{:S(2)}) %all-to-all-start.5) | async-done | bytes 524320 | tf_op jit(solution)/shard_map/all_to_all | solution.py:35
  120.4 0.2 fusion.7
  120.7 19.8 %all_to_all.62 = f32[16,1,64,128]{3,2,1,0:T(8,128)S(1)} all-to-all(f32[16,1,64,128]{3,2,1,0:T(8,128)S(1)} %broadcast_in_dim.26), channel_id=1, replica_groups=mesh['wide'=16,'narrow'=8,'grp'=2] {'wide'}, dimensions={0} | all-to-all | bytes 1048576 | tf_op jit(solution)/shard_map/all_to_all | solution.py:20
  140.6 4.6 %convolution_bitcast_fusion.1 = f32[1024,128]{0,1:T(8,128)S(1)} fusion(f32[1024,128]{1,0:T(8,128)S(1)} %bitcast.134, f32[1024,1024]{1,0:T(8,128)} %bitcast.129), kind=kOutput, calls=%fused_computation.4 | convolution fusion | flops 1610612736 | bytes 5242880 | tf_op jit(solution)/shard_map/dot_general | solution.py:93
  145.2 1.0 copy.36
  146.1 0.1 broadcast_in_dim.30
  146.3 7.5 %all_to_all.63 = f32[2,16,1,64,128]{4,3,1,2,0:T(8,128)S(1)} all-to-all(f32[2,16,1,64,128]{4,3,1,2,0:T(8,128)S(1)} %broadcast_in_dim.30), channel_id=1, replica_groups=mesh['wide'=16,'narrow'=8,'grp'=2] {'grp'}, dimensions={0} | all-to-all | bytes 2097152 | tf_op jit(solution)/shard_map/all_to_all | solution.py:20
  153.8 3.7 %all-to-all-start.8 = ((f32[16,64,128]{2,1,0:T(8,128)}), f32[16,64,128]{2,1,0:T(8,128)S(1)}, u32[]{:S(2)}, u32[]{:S(2)}) async-start(f32[16,64,128]{2,1,0:T(8,128)} %bitcast.33), calls=%async_computation.8 | async-start | bytes 1048576 | tf_op jit(solution)/shard_map/all_to_all | solution.py:35
  157.6 0.1 copy.37
  157.7 2.6 %gather_fusion.2 = f32[1536,128]{1,0:T(8,128)S(1)} fusion(f32[2048,128]{1,0:T(8,128)S(1)} %bitcast.124, s32[2048]{0:T(1024)S(1)} %pad_clamp_fusion), kind=kCustom, calls=%fused_computation.2.clone | custom fusion | bytes 1579008 | tf_op jit(solution)/shard_map/jit(_take)/gather | solution.py:104
  160.3 0.9 fusion.10
  161.2 6.1 %all-to-all-done.8 = f32[16,64,128]{2,1,0:T(8,128)S(1)} async-done(((f32[16,64,128]{2,1,0:T(8,128)}), f32[16,64,128]{2,1,0:T(8,128)S(1)}, u32[]{:S(2)}, u32[]{:S(2)}) %all-to-all-start.8) | async-done | bytes 524320 | tf_op jit(solution)/shard_map/all_to_all | solution.py:35
  167.3 0.2 fusion.9
  167.6 0.0 copy-start.2
  167.6 0.7 add_bitcast_fusion
  168.3 0.0 copy-done.2
  (13 shorter events, 0.3 us)
Async XLA Ops:
  0.6 16.6 %copy-start = (f32[1,48,1536]{2,1,0:T(8,128)S(1)}, f32[1,48,1536]{2,1,0:T(8,128)}, u32[]{:S(2)}) copy-start(f32[1,48,1536]{2,1,0:T(8,128)} %param.9) | copy-start | bytes 884740
  3.0 29.0 %all-to-all-start = ((f32[16,1,64,128]{3,2,1,0:T(8,128)}), f32[16,1,64,128]{3,2,1,0:T(8,128)S(1)}, u32[]{:S(2)}, u32[]{:S(2)}) async-start(f32[16,1,64,128]{3,2,1,0:T(8,128)} %broadcast_in_dim.22), calls=%async_computation | async-start | bytes 1048576 | tf_op jit(solution)/shard_map/all_to_all | solution.py:20
  32.0 20.3 %all-to-all-start.2 = ((f32[32,1,2,1536]{3,2,1,0:T(2,128)}), f32[32,1,2,1536]{3,2,1,0:T(2,128)S(1)}, u32[]{:S(2)}, u32[]{:S(2)}) async-start(f32[32,1,2,1536]{3,2,1,0:T(2,128)} %copy.29), calls=%async_computation.2 | async-start | bytes 786432 | tf_op jit(solution)/shard_map/all_to_all | solution.py:74
  58.2 14.5 %all-to-all-start.1 = ((f32[16,64,128]{2,1,0:T(8,128)}), f32[16,64,128]{2,1,0:T(8,128)S(1)}, u32[]{:S(2)}, u32[]{:S(2)}) async-start(f32[16,64,128]{2,1,0:T(8,128)} %bitcast.5), calls=%async_computation.1 | async-start | bytes 1048576 | tf_op jit(solution)/shard_map/all_to_all | solution.py:35
  63.7 9.0 %copy-start.1 = (f32[1,64,128]{2,1,0:T(8,128)S(1)}, f32[1,64,128]{2,1,0:T(8,128)}, u32[]{:S(2)}) copy-start(f32[1,64,128]{2,1,0:T(8,128)} %param.13) | copy-start | bytes 98308
  106.9 13.5 %all-to-all-start.5 = ((f32[16,64,128]{2,1,0:T(8,128)}), f32[16,64,128]{2,1,0:T(8,128)S(1)}, u32[]{:S(2)}, u32[]{:S(2)}) async-start(f32[16,64,128]{2,1,0:T(8,128)} %bitcast.23), calls=%async_computation.5 | async-start | bytes 1048576 | tf_op jit(solution)/shard_map/all_to_all | solution.py:35
  153.8 13.5 %all-to-all-start.8 = ((f32[16,64,128]{2,1,0:T(8,128)}), f32[16,64,128]{2,1,0:T(8,128)S(1)}, u32[]{:S(2)}, u32[]{:S(2)}) async-start(f32[16,64,128]{2,1,0:T(8,128)} %bitcast.33), calls=%async_computation.8 | async-start | bytes 1048576 | tf_op jit(solution)/shard_map/all_to_all | solution.py:35
  167.6 0.7 copy-start.2
where the time goes:
time: 169 us; the launch traced here: 168 us
  blocking collectives  61.3 us (36%)
  waiting for transfers between devices  38.1 us (23%)
  starting transfers between devices  30.2 us (18%)
  matrix products  18.1 us (11%)
  local copies, waits for them, and re-layouts  13.5 us (8%)
  other arithmetic  5.66 us (3%)
    all_to_all x5, blocking collectives, from_everyone(): return lax.all_to_all(copies, axis, split_axis=0, concat_axis=0, tiled=True)  61.3 us
    all_to_all x3, waiting for transfers between devices, summed_on_arrival(): lax.all_to_all(cut_along(value, dim, devices), axis, 0, 0, tiled=True)  17.7 us
    dot_general x3, matrix products, on_device(): lax.dot_general(tile_block, stacked, (((0,), (0,)), ((), ())), precision=...  13.7 us
    all_to_all x1, waiting for transfers between devices, from_everyone(): return lax.all_to_all(copies, axis, split_axis=0, concat_axis=0, tiled=True)  12.6 us
    all_to_all x3, starting transfers between devices, summed_on_arrival(): lax.all_to_all(cut_along(value, dim, devices), axis, 0, 0, tiled=True)  12.3 us
    all_to_all x1, starting transfers between devices, from_everyone(): return lax.all_to_all(copies, axis, split_axis=0, concat_axis=0, tiled=True)  11.7 us
    gather x3, local copies, waits for them, and re-layouts, on_device(): jnp.take(flat_panel, interface_rows, axis=0) * live_mask[:, :, None]  7.78 us
    all_to_all x1, waiting for transfers between devices, on_device(): lax.all_to_all(outgoing, ('wide', 'grp'), split_axis=0, concat_axis=0, ti...  7.75 us
  transfers between devices with their start and end apart: 5, of which 5 were waited for; matrix products, arithmetic and copies ran while one was open for 13% of the time, Pallas kernels for 0%

commit v1 on v0

v1 whole, which is shorter than its diff:
```python
import functools

import jax
import jax.numpy as jnp
from jax import lax
from jax.experimental import pallas as pl
from jax.experimental.pallas import tpu as pltpu
from jax.sharding import PartitionSpec as P

ITERS = 3
RELAX = 0.35
MESH = pl.DeviceIdType.MESH
NZ, NX = 8, 4

SLOTS = [
    (0, 0), (0, 1), (1, 0), (1, 1), (7, 0), (7, 1), (2, 0), (2, 1),
    (6, 0), (6, 1), (3, 0), (3, 1), (5, 0), (5, 1), (4, 0), (4, 1),
]
SLOT_OF = {v: i for i, v in enumerate(SLOTS)}
PARENT = {v: ((0, 0) if v[1] == 0 or v[0] == 0 else (v[0], 0)) for v in SLOTS if v != (0, 0)}
ROOT_ORDER = [(1, 0), (7, 0), (2, 0), (6, 0), (3, 0), (5, 0), (4, 0), (0, 1)]
PLAN = [
    (1, 0), (7, 0), (2, 0), (6, 0), (3, 0), (5, 0), (4, 0), (0, 1), (1, 1), 0,
    (7, 1), (2, 1), 1, (6, 1), (3, 1), 2, (5, 1), (4, 1), 3,
]
PAIRS = [(dx, dy) for dx in (2, 1, 3, 0) for dy in (1, 0) if (dx, dy) != (0, 0)]
FAR = [
    (dz, dy, dg)
    for dz in (4, 3, 5, 2, 6, 1, 7, 0)
    for dy in (1, 0)
    for dg in (1, 0)
    if (dz, dy, dg) != (0, 0, 0)
]


def halves(value):
    high = value.astype(jnp.bfloat16)
    low = (value - high.astype(jnp.float32)).astype(jnp.bfloat16)
    return high, low


def dot(a, b):
    return jnp.dot(a, b, preferred_element_type=jnp.float32)


def dot_t(a, b):
    return lax.dot_general(a, b, (((1,), (1,)), ((), ())), preferred_element_type=jnp.float32)


def kernel(
    bb, schur, q_row, q_blocks, live, scale, exc, out_t, out_r,
    bload, sboth, lhs_h, lhs_l, gath, part, from_core, to_pair, from_pair, to_far, from_far,
    keys, place, weight,
    load_sem, s_send, s_recv, g_send, g_recv, c_send, c_recv, p_send, p_recv, f_send, f_recv,
):
    wide, narrow, grp = lax.axis_index("wide"), lax.axis_index("narrow"), lax.axis_index("grp")
    z, yh, x, yl = wide // 2, wide % 2, narrow // 2, narrow % 2
    share = sboth.shape[1]
    iface = sboth.shape[2]
    extra = 2 * share

    def wide_at(dz, dy):
        return ((z + dz) % NZ) * 2 + (yh + dy) % 2

    def narrow_at(dx, dy):
        return ((x + dx) % NX) * 2 + (yl + dy) % 2

    def remote(src, dst, send, recv, device):
        return pltpu.make_async_remote_copy(
            src_ref=src, dst_ref=dst, send_sem=send, recv_sem=recv, device_id=device, device_id_type=MESH
        )

    barrier = pltpu.get_barrier_semaphore()
    for dz, dy, dg in FAR:
        pl.semaphore_signal(
            barrier, inc=1, device_id=(wide_at(dz, dy), narrow, (grp + dg) % 2), device_id_type=MESH
        )
    for dx, dy in PAIRS:
        pl.semaphore_signal(barrier, inc=1, device_id=(wide, narrow_at(dx, dy), grp), device_id_type=MESH)

    s_load = pltpu.make_async_copy(schur.at[0], sboth.at[grp], load_sem.at[16])
    s_load.start()
    b_loads = []
    for i, (dz, dy) in enumerate(SLOTS):
        source = ((z + NZ - dz) % NZ) * 2 + (yh + dy) % 2
        b_loads.append(pltpu.make_async_copy(bb.at[source], bload.at[i], load_sem.at[i]))
        b_loads[-1].start()

    forcing = exc[0]
    own = jnp.broadcast_to(scale[...], (64, 64))
    diagonal = lax.broadcasted_iota(jnp.int32, (64, 64), 0) == lax.broadcasted_iota(jnp.int32, (64, 64), 1)
    column = jnp.sum(jnp.where(diagonal, own, 0.0), axis=1, keepdims=True)
    weight[...] = jnp.broadcast_to(RELAX * column, (64, 128))
    gath[0, 0] = weight[...] * forcing
    live_count = live[0]

    pl.semaphore_wait(barrier, len(FAR) + len(PAIRS))

    def gather_copy(it, v):
        parent = PARENT[v]
        device = (wide_at(v[0] - parent[0], v[1] - parent[1] + 2), narrow, grp)
        k = SLOT_OF[v]
        return remote(
            gath.at[it, SLOT_OF[parent]], gath.at[it, k], g_send.at[it, k - 1], g_recv.at[it, k - 1], device
        )

    def hand_on(it, v):
        order = ROOT_ORDER if v == (0, 0) else SLOTS[1:]
        for child in order:
            if PARENT[child] == v:
                gather_copy(it, child).start()

    hand_on(0, (0, 0))
    s_load.wait()
    s_copy = remote(sboth.at[grp], sboth.at[grp], s_send, s_recv, (wide, narrow, 1 - grp))
    s_copy.start()

    def split_block(c):
        for i in range(4 * c, 4 * c + 4):
            b_loads[i].wait()
        for h in range(2):
            i = 4 * c + 2 * h
            block = bload[i : i + 2].reshape(128, bload.shape[2])
            for m in range(0, block.shape[1], 256):
                high, low = halves(block[:, m : m + 256].T)
                lhs_h[c, pl.ds(extra + m, 256), pl.ds(128 * h, 128)] = high
                lhs_l[c, pl.ds(extra + m, 256), pl.ds(128 * h, 128)] = low

    def split_schur(c):
        q = q_row[...]
        lane = lax.broadcasted_iota(jnp.int32, (1, iface), 1)
        q = jnp.where(lane < live_count, q, -1)
        rows = []
        for i in range(4 * c, 4 * c + 4):
            dz, dy = SLOTS[i]
            source = ((z + NZ - dz) % NZ) * 2 + (yh + dy) % 2
            shifted = jnp.broadcast_to(q - (source * 128 + grp * 64), (64, iface))
            hit = shifted == lax.broadcasted_iota(jnp.int32, (64, iface), 0)
            rows.append(jnp.where(hit, 1.0, 0.0).astype(jnp.bfloat16))
        picked = jnp.concatenate(rows, axis=0)
        high, low = halves(sboth[...].reshape(extra, iface))
        lhs_h[c, 0:extra, :] = dot_t(high, picked).astype(jnp.bfloat16)
        lhs_l[c, 0:extra, :] = dot_t(low, picked).astype(jnp.bfloat16)

    def index_tables():
        q = q_blocks[...]
        blocks = q.shape[0]
        lane = lax.broadcasted_iota(jnp.int32, (blocks, 128), 1)
        block = lax.broadcasted_iota(jnp.int32, (blocks, 128), 0)
        owner = q // 64
        rank = jnp.zeros_like(q)
        for d in range(1, share):
            same = (pltpu.roll(owner, d, 1) == owner) & (lane >= d)
            rank = rank + jnp.where(same, 1, 0)
        used = (lane < share) & (block * share + lane < live_count)
        core = block % 2
        keys[...] = jnp.where(used, owner * 4 + core * 2 + rank, -1)
        mine = used & (owner == wide * 2 + grp)
        rowpos = jnp.zeros((1, 128), jnp.int32)
        for level in range(2):
            spot = jnp.where(mine & (rank == level), q % 64 + 1, 0)
            spot = jnp.sum(spot, axis=1, keepdims=True)
            match = (block == 2 * (lane // 8) + (lane % 4) // 2) & (lane % 2 == level)
            rowpos = rowpos + jnp.sum(jnp.where(match, spot, 0), axis=0, keepdims=True)
        row = lax.broadcasted_iota(jnp.int32, (64, 128), 0)
        place[...] = jnp.where(row == rowpos - 1, 1.0, 0.0).astype(jnp.bfloat16)

    def multiply(it, c):
        high, low = halves(gath[it, 4 * c : 4 * c + 4].reshape(256, 128))
        both = jnp.concatenate([high, low], axis=1)
        wide_part = dot(lhs_h[c], both)
        total = wide_part[:, 0:128] + wide_part[:, 128:256] + dot(lhs_l[c], high)
        if c == 0:
            part[it] = total
        else:
            part[it] = part[it] + total

    def far_copy(it, k):
        dz, dy, dg = FAR[k]
        target, core = wide_at(dz, dy), (grp + dg) % 2
        return remote(
            to_far.at[it, target * 2 + core], from_far.at[it, wide * 2 + grp],
            f_send.at[it, k], f_recv.at[it, k], (target, narrow, core),
        )

    def core_copy(it, k):
        dx, dy = (PAIRS + [(0, 0)])[k]
        row = pl.multiple_of(extra + narrow_at(dx, dy) * 128 + (1 - grp) * 64, 32)
        return remote(
            part.at[it, pl.ds(row, 64)], from_core.at[it, k], c_send.at[it, k], c_recv.at[it, k],
            (wide, narrow, 1 - grp),
        )

    def pair_copy(it, k):
        dx, dy = PAIRS[k]
        return remote(
            to_pair.at[it, k], from_pair.at[it, k], p_send.at[it, k], p_recv.at[it, k],
            (wide, narrow_at(dx, dy), grp),
        )

    def sweep(it, first):
        if first:
            chores = [
                functools.partial(split_block, 0), functools.partial(split_block, 1), index_tables,
                functools.partial(split_block, 2), functools.partial(split_block, 3), s_copy.wait,
                functools.partial(split_schur, 0), functools.partial(split_schur, 1),
                functools.partial(split_schur, 2), functools.partial(split_schur, 3),
            ]
        else:
            chores = []
        for step in PLAN:
            if isinstance(step, tuple):
                if chores:
                    chores.pop(0)()
                gather_copy(it, step).wait_recv()
                hand_on(it, step)
            else:
                while chores:
                    chores.pop(0)()
                multiply(it, step)
        for k in range(len(PAIRS) + 1):
            core_copy(it, k).start()
        outgoing = jnp.zeros((128, 256), jnp.float32)
        for core in range(2):
            key = keys[pl.ds(2 * wide + core, 1), :]
            row = lax.broadcasted_iota(jnp.int32, (128, 128), 0)
            pick = jnp.where(row == key, 1.0, 0.0).astype(jnp.bfloat16)[:, 0:share]
            high, low = halves(part[it, core * share : (core + 1) * share])
            outgoing = outgoing + dot(pick, jnp.concatenate([high, low], axis=1))
        outgoing = (outgoing[:, 0:128] + outgoing[:, 128:256]).reshape(32, 4, 128)
        to_far[it] = outgoing
        for k in range(len(FAR)):
            far_copy(it, k).start()
        from_far[it, wide * 2 + grp] = to_far[it, wide * 2 + grp]
        for k in range(len(PAIRS) + 1):
            dx, dy = (PAIRS + [(0, 0)])[k]
            row = pl.multiple_of(extra + narrow_at(dx, dy) * 128 + grp * 64, 32)
            core_copy(it, k).wait_recv()
            value = part[it, pl.ds(row, 64)] + from_core[it, k]
            if k < len(PAIRS):
                to_pair[it, k] = value
                pair_copy(it, k).start()
            else:
                total = value
        for k in range(len(FAR)):
            far_copy(it, k).wait_recv()
        high, low = halves(from_far[it].reshape(128, 128))
        landed = dot(place[...], jnp.concatenate([high, low], axis=1))
        total = total + (landed[:, 0:128] + landed[:, 128:256])
        for k in range(len(PAIRS)):
            pair_copy(it, k).wait_recv()
            total = total + from_pair[it, k]
        residual = exc[0] - total
        out_r[0] = residual
        updated = gath[it, 0] + weight[...] * residual
        out_t[0] = updated
        return updated

    def finish(it):
        for v in SLOTS[1:]:
            gather_copy(it, v).wait_send()
        for k in range(len(PAIRS) + 1):
            core_copy(it, k).wait_send()
        for k in range(len(FAR)):
            far_copy(it, k).wait_send()
        for k in range(len(PAIRS)):
            pair_copy(it, k).wait_send()

    gath[1, 0] = sweep(0, True)
    hand_on(1, (0, 0))

    def later(it, carry):
        updated = sweep(it, False)

        @pl.when(it < ITERS - 1)
        def _():
            gath[it + 1, 0] = updated
            hand_on(it + 1, (0, 0))

        return carry

    lax.fori_loop(1, ITERS, later, 0)
    lax.fori_loop(0, ITERS, lambda it, carry: (finish(it), carry)[1], 0)


def on_device(boundary_block, schur_blocks, interface_rows, live_rows, row_scale, excitation):
    slots, piece, columns = boundary_block.shape
    share, iface = schur_blocks.shape[1:]
    rows = 2 * share + columns
    blocks = iface // share
    q_blocks = jnp.pad(interface_rows.reshape(blocks, share), ((0, 0), (0, 128 - share)))
    f32, dma = jnp.float32, pltpu.SemaphoreType.DMA
    vmem = pl.BlockSpec(memory_space=pltpu.VMEM)
    hbm = pl.BlockSpec(memory_space=pl.ANY)
    pairs = len(PAIRS)
    return pl.pallas_call(
        kernel,
        out_shape=(
            jax.ShapeDtypeStruct(excitation.shape, f32),
            jax.ShapeDtypeStruct(excitation.shape, f32),
        ),
        in_specs=[hbm, hbm, vmem, vmem, pl.BlockSpec(memory_space=pltpu.SMEM), vmem, vmem],
        out_specs=(vmem, vmem),
        scratch_shapes=[
            pltpu.VMEM((slots, piece, columns), f32),
            pltpu.VMEM((2, share, iface), f32),
            pltpu.VMEM((4, rows, 256), jnp.bfloat16),
            pltpu.VMEM((4, rows, 256), jnp.bfloat16),
            pltpu.VMEM((ITERS, slots, piece, 128), f32),
            pltpu.VMEM((ITERS, rows, 128), f32),
            pltpu.VMEM((ITERS, pairs + 1, piece, 128), f32),
            pltpu.VMEM((ITERS, pairs, piece, 128), f32),
            pltpu.VMEM((ITERS, pairs, piece, 128), f32),
            pltpu.VMEM((ITERS, blocks, 4, 128), f32),
            pltpu.VMEM((ITERS, blocks, 4, 128), f32),
            pltpu.VMEM((blocks, 128), jnp.int32),
            pltpu.VMEM((piece, 128), jnp.bfloat16),
            pltpu.VMEM((piece, 128), f32),
            dma((slots + 1,)),
            dma(()),
            dma(()),
            dma((ITERS, slots - 1)),
            dma((ITERS, slots - 1)),
            dma((ITERS, pairs + 1)),
            dma((ITERS, pairs + 1)),
            dma((ITERS, pairs)),
            dma((ITERS, pairs)),
            dma((ITERS, len(FAR))),
            dma((ITERS, len(FAR))),
        ],
        name="sweeps",
        compiler_params=pltpu.CompilerParams(collective_id=0, has_side_effects=True),
    )(boundary_block, schur_blocks, interface_rows, q_blocks, live_rows, row_scale, excitation)


def solution(mesh):
    placed = (
        P(None, ("narrow", "grp"), "wide"),
        P("narrow", ("wide", "grp"), None),
        P("narrow", None),
        P("narrow"),
        P("wide", ("narrow", "grp")),
        P("wide", ("narrow", "grp"), None),
    )
    return jax.shard_map(
        on_device,
        mesh=mesh,
        in_specs=placed,
        out_specs=(P("wide", ("narrow", "grp"), None), P("wide", ("narrow", "grp"), None)),
        check_vma=False,
    )
```

time: 169 us -> 81.8 us (0.48)
  Pallas kernels: 0 us -> 76 us
  blocking collectives: 61.3 us -> 0 us
  waiting for transfers between devices: 38.1 us -> 0 us
  starting transfers between devices: 30.2 us -> 0 us
  matrix products: 18.1 us -> 0 us
  local copies, waits for them, and re-layouts: 13.5 us -> 3.44 us
  other arithmetic: 5.66 us -> 0.71 us
    pallas_call x0 -> x1, Pallas kernels: none -> 76 us  [on_device(): pl.pallas_call(kernel, out_shape=(jax.ShapeDtypeStruct(excitation.shape,...]
    all_to_all x5 -> x0, blocking collectives: 61.3 us -> none  [from_everyone(): return lax.all_to_all(copies, axis, split_axis=0, concat_axis=0, tiled=True)]
    all_to_all x5 -> x0, waiting for transfers between devices: 38.1 us -> none  [the longest x3 17.7 us: summed_on_arrival(): lax.all_to_all(cut_along(value, dim, devices), axis, 0, 0, tiled=True)]
    all_to_all x5 -> x0, starting transfers between devices: 30.2 us -> none  [the longest x3 12.3 us: summed_on_arrival(): lax.all_to_all(cut_along(value, dim, devices), axis, 0, 0, tiled=True)]
    dot_general x11 -> x0, matrix products: 18.1 us -> none  [the longest x3 13.7 us: on_device(): lax.dot_general(tile_block, stacked, (((0,), (0,)), ((), ())), precision=...]
    gather x3 -> x0, local copies, waits for them, and re-layouts: 7.78 us -> none  [on_device(): jnp.take(flat_panel, interface_rows, axis=0) * live_mask[:, :, None]]
    dot_general x3 -> x0, local copies, waits for them, and re-layouts: 2.97 us -> none  [on_device(): lax.dot_general(tile_block, stacked, (((0,), (0,)), ((), ())), precision=...]
    unnamed x6 -> x2, local copies, waits for them, and re-layouts: 0.02 us -> 2.75 us
  transfers between devices with their start and end apart: 5 -> 0, of which waited for: 5 -> 0; matrix products, arithmetic and copies ran while one was open for 13% -> 0% of each run, Pallas kernels for 0% -> 0%
where the time goes in v1:
time: 81.8 us; the launch traced here: 81.5 us
  Pallas kernels  76 us (93%)
  local copies, waits for them, and re-layouts  3.44 us (4%)
  between operations  1.29 us (2%)
    pallas_call x1, Pallas kernels, on_device(): pl.pallas_call(kernel, out_shape=(jax.ShapeDtypeStruct(excitation.shape,...  76 us
    unnamed x2, local copies, waits for them, and re-layouts  2.75 us

profile of v1, /device:TPU:1, one launch (start us, length us, event | category | flops | bytes accessed | tf_op | source)
XLA Modules:
  0.0 81.5 jit_solution(3267503454989373867)
XLA Ops:
  1.3 0.7 reduce
  2.0 0.1 reshape.7
  2.1 0.6 pad.4.q_blocks
  2.7 76.0 %sweeps.1 = (f32[1,64,128]{2,1,0:T(8,128)}, f32[1,64,128]{2,1,0:T(8,128)}) custom-call(f32[16,64,1024]{2,1,0:T(8,128)} %bb.1, f32[1,48,1536]{2,1,0:T(8,128)} %schur.1, s32[1,1536]{1,0:T(1,128)} %q_row.1, s32[32,128]{1,0:T(8,128)} %pad.4.q_blocks, s32[1]{0:T(128)S(6)} %copy.10.live, f32[1,64]{1,0:T(1,128)} %scale.1, f32[1,64,128]{2,1,0:T(8,128)} %exc.1), custom_call_target="tpu_custom_call" | custom-call | tf_op jit(solution)/shard_map/sweeps/pallas_call | solution.py:296
  78.7 1.4 %copy.11 = f32[1,64,128]{2,1,0:T(8,128)} copy(f32[1,64,128]{2,1,0:T(8,128)} %get-tuple-element.4) | data formatting | bytes 65536
  80.1 1.4 %copy.12 = f32[1,64,128]{2,1,0:T(8,128)} copy(f32[1,64,128]{2,1,0:T(8,128)} %get-tuple-element.5) | data formatting | bytes 65536

commit v2 on v1

v2 whole, which is shorter than its diff:
```python
import functools

import jax
import jax.numpy as jnp
from jax import lax
from jax.experimental import pallas as pl
from jax.experimental.pallas import tpu as pltpu
from jax.sharding import PartitionSpec as P

ITERS = 3
RELAX = 0.35
MESH = pl.DeviceIdType.MESH
NZ, NX = 8, 4

SLOTS = [(0, 0), (4, 1), (3, 1), (5, 1), (2, 1), (6, 1), (1, 1), (7, 1)]
SLOTS += [(4, 0), (3, 0), (5, 0), (2, 0), (6, 0), (1, 0), (7, 0), (0, 1)]
SLOT_OF = {v: i for i, v in enumerate(SLOTS)}
PAIRS = [(dx, dy, dg) for dy in (1, 0) for dx in (2, 1, 3, 0) for dg in (1, 0) if (dx, dy, dg) != (0, 0, 0)]
FAR = [
    (dz, dy, dg)
    for dz in (4, 3, 5, 2, 6, 1, 7, 0)
    for dy in (1, 0)
    for dg in (1, 0)
    if (dz, dy, dg) != (0, 0, 0)
]


def halves(value):
    high = value.astype(jnp.bfloat16)
    low = (value - high.astype(jnp.float32)).astype(jnp.bfloat16)
    return high, low


def dot(a, b):
    return jnp.dot(a, b, preferred_element_type=jnp.float32)


def dot_t(a, b):
    return lax.dot_general(a, b, (((1,), (1,)), ((), ())), preferred_element_type=jnp.float32)


def kernel(
    bb, schur, q_row, live, scale, exc, out,
    bload, sboth, lhs, gath, acc, part, from_pair, to_far, from_far,
    q_blocks, keys, place, weight, force, left,
    load_sem, s_send, s_recv, g_send, g_recv, p_send, p_recv, f_send, f_recv,
):
    wide, narrow, grp = lax.axis_index("wide"), lax.axis_index("narrow"), lax.axis_index("grp")
    z, yh, x, yl = wide // 2, wide % 2, narrow // 2, narrow % 2
    share = sboth.shape[1]
    iface = sboth.shape[2]
    extra = 2 * share
    me = wide * 2 + grp
    left_lanes = lax.broadcasted_iota(jnp.int32, (32, 128), 1) < 64

    def wide_at(dz, dy):
        return ((z + dz + NZ) % NZ) * 2 + (yh + dy + 2) % 2

    def narrow_at(dx, dy):
        return ((x + dx) % NX) * 2 + (yl + dy) % 2

    def swap(value):
        return pltpu.roll(value, 64, 1)

    def remote(src, dst, send, recv, device):
        return pltpu.make_async_remote_copy(
            src_ref=src, dst_ref=dst, send_sem=send, recv_sem=recv, device_id=device, device_id_type=MESH
        )

    barrier = pltpu.get_barrier_semaphore()
    for dz, dy, dg in FAR:
        pl.semaphore_signal(
            barrier, inc=1, device_id=(wide_at(dz, dy), narrow, (grp + dg) % 2), device_id_type=MESH
        )
    for dx, dy, dg in PAIRS[:-1]:
        pl.semaphore_signal(
            barrier, inc=1, device_id=(wide, narrow_at(dx, dy), (grp + dg) % 2), device_id_type=MESH
        )

    b_loads = []
    for i, (dz, dy) in enumerate(SLOTS):
        b_loads.append(pltpu.make_async_copy(bb.at[wide_at(-dz, dy)], bload.at[i], load_sem.at[i]))
        b_loads[-1].start()
    s_load = pltpu.make_async_copy(schur.at[0], sboth.at[grp], load_sem.at[len(SLOTS)])
    s_load.start()

    own = jnp.broadcast_to(scale[...], (64, 64))
    diagonal = lax.broadcasted_iota(jnp.int32, (64, 64), 0) == lax.broadcasted_iota(jnp.int32, (64, 64), 1)
    column = RELAX * jnp.sum(jnp.where(diagonal, own, 0.0), axis=1, keepdims=True)
    weight[...] = jnp.where(
        left_lanes, jnp.broadcast_to(column[0:32], (32, 128)), jnp.broadcast_to(column[32:64], (32, 128))
    )
    upper, lower = exc[0, 0:32], exc[0, 32:64]
    force[0] = jnp.where(left_lanes, upper, swap(lower))
    force[1] = jnp.where(left_lanes, swap(upper), lower)
    for h in range(2):
        gath[0, h, 0] = weight[...] * force[h]
    live_count = live[0]

    def gather_copy(it, h, k):
        dz, dy = SLOTS[k]
        return remote(
            gath.at[it, h, 0], gath.at[it, h, k], g_send.at[it, h], g_recv.at[it, h, k - 1],
            (wide_at(dz, dy), narrow, grp),
        )

    def hand_out(it, h):
        for k in range(1, len(SLOTS)):
            gather_copy(it, h, k).start()

    def split_block(c):
        for i in range(4 * c, 4 * c + 4):
            b_loads[i].wait()
        for pair in range(2):
            i = 4 * c + 2 * pair
            block = bload[i : i + 2].reshape(128, bload.shape[2])
            for m in range(0, block.shape[1], 256):
                high, low = halves(block[:, m : m + 256].T)
                lhs[c, pl.ds(extra + m, 256), pl.ds(128 * pair, 128)] = high
                lhs[c, pl.ds(extra + m, 256), pl.ds(256 + 128 * pair, 128)] = low

    def split_schur(c):
        q = q_row[...]
        lane = lax.broadcasted_iota(jnp.int32, (1, iface), 1)
        q = jnp.where(lane < live_count, q, -1)
        rows = []
        for i in range(4 * c, 4 * c + 4):
            dz, dy = SLOTS[i]
            shifted = jnp.broadcast_to(q - (wide_at(-dz, dy) * 128 + grp * 64), (64, iface))
            hit = shifted == lax.broadcasted_iota(jnp.int32, (64, iface), 0)
            rows.append(jnp.where(hit, 1.0, 0.0).astype(jnp.bfloat16))
        picked = jnp.concatenate(rows, axis=0)
        high, low = halves(sboth[...].reshape(extra, iface))
        lhs[c, 0:extra, 0:256] = dot_t(high, picked).astype(jnp.bfloat16)
        lhs[c, 0:extra, 256:512] = dot_t(low, picked).astype(jnp.bfloat16)

    def index_tables():
        blocks = q_blocks.shape[0]
        for b in range(blocks):
            q_blocks[b : b + 1, 0:share] = q_row[:, b * share : (b + 1) * share]
        q = q_blocks[...]
        lane = lax.broadcasted_iota(jnp.int32, (blocks, 128), 1)
        block = lax.broadcasted_iota(jnp.int32, (blocks, 128), 0)
        owner = q // 64
        rank = jnp.zeros_like(q)
        for d in range(1, share):
            same = (pltpu.roll(owner, d, 1) == owner) & (lane >= d)
            rank = rank + jnp.where(same, 1, 0)
        used = (lane < share) & (block * share + lane < live_count)
        keys[...] = jnp.where(used, owner + 32 * rank, -1)
        mine = used & (owner == me)
        row = lax.broadcasted_iota(jnp.int32, (64, 128), 0)
        for level in range(2):
            spot = jnp.where(mine & (rank == level), q % 64 + 1, 0)
            spot = jnp.sum(spot, axis=1, keepdims=True)
            match = (block == 2 * (lane // 4) + lane % 2) & (lane < 64)
            rowpos = jnp.sum(jnp.where(match, spot, 0), axis=0, keepdims=True)
            place[64 * level : 64 * level + 64] = jnp.where(row == rowpos - 1, 1.0, 0.0).astype(jnp.bfloat16)

    def right_side(it, h, c):
        rows = []
        for i in range(4 * c, 4 * c + 4):
            value = gath[it, h, i]
            high = value.astype(jnp.bfloat16).astype(jnp.float32)
            low = value - high
            rows.append(jnp.where(left_lanes, high, swap(low)))
            rows.append(jnp.where(left_lanes, swap(high), low))
        right = jnp.concatenate(rows, axis=0).astype(jnp.bfloat16)
        return jnp.concatenate([right, right], axis=0)

    def multiply(it, h, c):
        total = dot(lhs[c], right_side(it, h, c))
        if c == 0:
            acc[h] = total
        else:
            acc[h] = acc[h] + total

    def far_copy(it, h, k):
        dz, dy, dg = FAR[k]
        target, core = wide_at(dz, dy), (grp + dg) % 2
        return remote(
            to_far.at[it, h, target * 2 + core], from_far.at[it, h, me],
            f_send.at[it, h], f_recv.at[it, h], (target, narrow, core),
        )

    def pair_copy(it, h, k):
        dx, dy, dg = PAIRS[k]
        target, core = narrow_at(dx, dy), (grp + dg) % 2
        return remote(
            part.at[it, h, target * 2 + core], from_pair.at[it, h, k], p_send.at[it, h], p_recv.at[it, h],
            (wide, target, core),
        )

    def send_far(it, h):
        packed = []
        for core in range(2):
            key = keys[pl.ds(2 * wide + core, 1), :]
            row = lax.broadcasted_iota(jnp.int32, (64, 128), 0)
            pick = jnp.where(row == key, 1.0, 0.0).astype(jnp.bfloat16)[:, 0:share]
            value = acc[h, core * share : (core + 1) * share]
            high = value.astype(jnp.bfloat16)
            low = (value - high.astype(jnp.float32)).astype(jnp.bfloat16)
            picked = dot(pick, jnp.concatenate([high, low], axis=1))
            picked = picked[:, 0:128] + picked[:, 128:256]
            picked = picked + swap(picked)
            packed.append(jnp.where(left_lanes, picked[0:32], picked[32:64]))
        to_far[it, h] = jnp.stack(packed, axis=1)
        for k in range(len(FAR)):
            far_copy(it, h, k).start()
        from_far[it, h, me] = to_far[it, h, me]

    def last_multiply(it, h):
        c = len(SLOTS) // 4 - 1
        right = right_side(it, h, c)
        acc[h, 0:extra] = acc[h, 0:extra] + dot(lhs[c, 0:extra], right)
        send_far(it, h)
        total = acc[h, extra:] + dot(lhs[c, extra:], right)
        total = total + swap(total)
        for b in range(16):
            part[it, h, b] = jnp.where(left_lanes, total[64 * b : 64 * b + 32], total[64 * b + 32 : 64 * b + 64])
        for k in range(len(PAIRS)):
            pair_copy(it, h, k).start()

    def update(it, h):
        here = (wide, narrow, grp)
        remote(
            from_pair.at[it, h], from_pair.at[it, h], p_send.at[it, h], p_recv.at[it, h], here
        ).wait_recv()
        total = part[it, h, narrow * 2 + grp]
        for k in range(len(PAIRS)):
            total = total + from_pair[it, h, k]
        far = len(FAR)
        remote(
            to_far.at[it, h, 0:far], from_far.at[it, h, 0:far], f_send.at[it, h], f_recv.at[it, h],
            (wide, narrow, grp),
        ).wait_recv()
        high, low = halves(from_far[it, h].reshape(64, 128))
        landed = dot(place[:, 0:64], jnp.concatenate([high, low], axis=1))
        landed = landed[:, 0:128] + landed[:, 128:256]
        one = jnp.where(left_lanes, landed[0:32], landed[96:128])
        two = jnp.where(left_lanes, landed[32:64], landed[64:96])
        residual = force[h] - (total + one + swap(two))
        updated = gath[it, h, 0] + weight[...] * residual
        return residual, updated

    def strip(it, h):
        for c in range(len(SLOTS) // 4):
            for k in range(max(4 * c, 1), 4 * c + 4):
                gather_copy(it, h, k).wait_recv()
            if 4 * c + 4 < len(SLOTS):
                multiply(it, h, c)
            else:
                last_multiply(it, h)

    def sweep(it, then):
        for h in range(2):
            strip(it, h)
        for h in range(2):
            then(it, h, *update(it, h))

    def go_on(it, h, residual, updated):
        gath[it + 1, h, 0] = updated
        hand_out(it + 1, h)

    def keep(it, h, residual, updated):
        force[h] = residual
        left[h] = updated

    def finish(it, carry):
        for h in range(2):
            here = (wide, narrow, grp)
            remote(
                gath.at[it, h, 1:], gath.at[it, h, 1:], g_send.at[it, h], g_recv.at[it, h, 0], here
            ).wait_send()
            remote(
                from_pair.at[it, h], from_pair.at[it, h], p_send.at[it, h], p_recv.at[it, h], here
            ).wait_send()
            far = len(FAR)
            remote(
                to_far.at[it, h, 0:far], from_far.at[it, h, 0:far], f_send.at[it, h], f_recv.at[it, h], here
            ).wait_send()
        return carry

    index_tables()
    split_block(0)
    split_block(1)
    pl.semaphore_wait(barrier, len(FAR) + len(PAIRS) - 1)
    hand_out(0, 0)
    hand_out(0, 1)
    s_load.wait()
    s_copy = remote(sboth.at[grp], sboth.at[grp], s_send, s_recv, (wide, narrow, 1 - grp))
    s_copy.start()
    chores = [functools.partial(split_block, 2), functools.partial(split_block, 3), s_copy.wait]
    chores += [functools.partial(split_schur, c) for c in range(4)]
    for chore in chores:
        chore()
    sweep(0, go_on)

    def middle(it, carry):
        sweep(it, go_on)
        return carry

    lax.fori_loop(1, ITERS - 1, middle, 0)
    sweep(ITERS - 1, keep)
    for i, value in enumerate((left, force)):
        out[i, 0:32] = jnp.where(left_lanes, value[0], swap(value[1]))
        out[i, 32:64] = jnp.where(left_lanes, swap(value[0]), value[1])
    lax.fori_loop(0, ITERS, finish, 0)


def on_device(boundary_block, schur_blocks, interface_rows, live_rows, row_scale, excitation):
    slots, piece, columns = boundary_block.shape
    share, iface = schur_blocks.shape[1:]
    rows = 2 * share + columns
    blocks = iface // share
    f32, dma = jnp.float32, pltpu.SemaphoreType.DMA
    vmem = pl.BlockSpec(memory_space=pltpu.VMEM)
    hbm = pl.BlockSpec(memory_space=pl.ANY)
    pairs = len(PAIRS)
    both = pl.pallas_call(
        kernel,
        out_shape=jax.ShapeDtypeStruct((2, piece, 128), f32),
        in_specs=[hbm, hbm, vmem, pl.BlockSpec(memory_space=pltpu.SMEM), vmem, vmem],
        out_specs=vmem,
        scratch_shapes=[
            pltpu.VMEM((slots, piece, columns), f32),
            pltpu.VMEM((2, share, iface), f32),
            pltpu.VMEM((slots // 4, rows, 512), jnp.bfloat16),
            pltpu.VMEM((ITERS, 2, slots, piece // 2, 128), f32),
            pltpu.VMEM((2, rows, 128), f32),
            pltpu.VMEM((ITERS, 2, slots, piece // 2, 128), f32),
            pltpu.VMEM((ITERS, 2, pairs, piece // 2, 128), f32),
            pltpu.VMEM((ITERS, 2, blocks, 2, 128), f32),
            pltpu.VMEM((ITERS, 2, blocks, 2, 128), f32),
            pltpu.VMEM((blocks, 128), jnp.int32),
            pltpu.VMEM((blocks, 128), jnp.int32),
            pltpu.VMEM((2 * piece, 128), jnp.bfloat16),
            pltpu.VMEM((piece // 2, 128), f32),
            pltpu.VMEM((2, piece // 2, 128), f32),
            pltpu.VMEM((2, piece // 2, 128), f32),
            dma((slots + 1,)),
            dma(()),
            dma(()),
            dma((ITERS, 2)),
            dma((ITERS, 2, slots - 1)),
            dma((ITERS, 2)),
            dma((ITERS, 2)),
            dma((ITERS, 2)),
            dma((ITERS, 2)),
        ],
        name="sweeps",
        compiler_params=pltpu.CompilerParams(collective_id=0, has_side_effects=True),
    )(boundary_block, schur_blocks, interface_rows, live_rows, row_scale, excitation)
    return both[0:1], both[1:2]


def solution(mesh):
    placed = (
        P(None, ("narrow", "grp"), "wide"),
        P("narrow", ("wide", "grp"), None),
        P("narrow", None),
        P("narrow"),
        P("wide", ("narrow", "grp")),
        P("wide", ("narrow", "grp"), None),
    )
    return jax.shard_map(
        on_device,
        mesh=mesh,
        in_specs=placed,
        out_specs=(P("wide", ("narrow", "grp"), None), P("wide", ("narrow", "grp"), None)),
        check_vma=False,
    )
```

time: 81.8 us -> 73.7 us (0.901)
  Pallas kernels: 76 us -> 70.8 us
  local copies, waits for them, and re-layouts: 3.44 us -> 1.4 us
    pallas_call x1, Pallas kernels: 76 us -> 70.8 us  [on_device(): pl.pallas_call(kernel, out_shape=jax.ShapeDtypeStruct((2, piece, 128), f3...]
    unnamed x2 -> x0, local copies, waits for them, and re-layouts: 2.75 us -> none
    slice x0 -> x1, local copies, waits for them, and re-layouts: none -> 1.4 us  [on_device(): return (both[0:1], both[1:2])]
where the time goes in v2:
time: 73.7 us; the launch traced here: 73.5 us
  Pallas kernels  70.8 us (96%)
  local copies, waits for them, and re-layouts  1.4 us (2%)
  between operations  1.29 us (2%)
    pallas_call x1, Pallas kernels, on_device(): pl.pallas_call(kernel, out_shape=jax.ShapeDtypeStruct((2, piece, 128), f3...  70.8 us

profile of v2, /device:TPU:1, one launch (start us, length us, event | category | flops | bytes accessed | tf_op | source)
XLA Modules:
  0.0 73.5 jit_solution(18193836404176945466)
XLA Ops:
  1.3 70.8 %sweeps.1 = f32[2,64,128]{2,1,0:T(8,128)} custom-call(f32[16,64,1024]{2,1,0:T(8,128)} %bb.1, f32[1,48,1536]{2,1,0:T(8,128)} %schur.1, s32[1,1536]{1,0:T(1,128)} %q_row.1, s32[1]{0:T(128)S(6)} %copy.8.live, f32[1,64]{1,0:T(1,128)} %scale.1, f32[1,64,128]{2,1,0:T(8,128)} %exc.1), custom_call_target="tpu_custom_call" | custom-call | tf_op jit(solution)/shard_map/sweeps/pallas_call | solution.py:320
  72.1 1.4 %fusion = (f32[1,64,128]{2,1,0:T(8,128)}, f32[1,64,128]{2,1,0:T(8,128)}) fusion(f32[2,64,128]{2,1,0:T(8,128)} %sweeps.1), kind=kLoop, calls=%fused_computation | loop fusion | bytes 131072 | tf_op jit(solution)/shard_map/slice | solution.py:354

commit v3 on v2

--- a/solution.py
+++ b/solution.py
@@ -40,9 +40,9 @@
 
 
 def kernel(
-    bb, schur, q_row, live, scale, exc, out,
+    bb, schur, q_hbm, live, scale_hbm, exc_hbm, out,
     bload, sboth, lhs, gath, acc, part, from_pair, to_far, from_far,
-    q_blocks, keys, place, weight, force, left,
+    q_row, scale, exc, q_blocks, keys, place, weight, force, left,
     load_sem, s_send, s_recv, g_send, g_recv, p_send, p_recv, f_send, f_recv,
 ):
     wide, narrow, grp = lax.axis_index("wide"), lax.axis_index("narrow"), lax.axis_index("grp")
@@ -67,6 +67,12 @@
             src_ref=src, dst_ref=dst, send_sem=send, recv_sem=recv, device_id=device, device_id_type=MESH
         )
 
+    small = [
+        pltpu.make_async_copy(src, dst, load_sem.at[len(SLOTS) + 1 + i])
+        for i, (src, dst) in enumerate(((exc_hbm, exc), (scale_hbm, scale), (q_hbm, q_row)))
+    ]
+    for copy in small:
+        copy.start()
     barrier = pltpu.get_barrier_semaphore()
     for dz, dy, dg in FAR:
         pl.semaphore_signal(
@@ -84,6 +90,8 @@
     s_load = pltpu.make_async_copy(schur.at[0], sboth.at[grp], load_sem.at[len(SLOTS)])
     s_load.start()
 
+    for copy in small:
+        copy.wait()
     own = jnp.broadcast_to(scale[...], (64, 64))
     diagonal = lax.broadcasted_iota(jnp.int32, (64, 64), 0) == lax.broadcasted_iota(jnp.int32, (64, 64), 1)
     column = RELAX * jnp.sum(jnp.where(diagonal, own, 0.0), axis=1, keepdims=True)
@@ -214,21 +222,20 @@
         right = right_side(it, h, c)
         acc[h, 0:extra] = acc[h, 0:extra] + dot(lhs[c, 0:extra], right)
         send_far(it, h)
-        total = acc[h, extra:] + dot(lhs[c, extra:], right)
-        total = total + swap(total)
-        for b in range(16):
-            part[it, h, b] = jnp.where(left_lanes, total[64 * b : 64 * b + 32], total[64 * b + 32 : 64 * b + 64])
-        for k in range(len(PAIRS)):
-            pair_copy(it, h, k).start()
+        for dx in (2, 1, 3, 0):
+            target = (x + dx) % NX
+            row = pl.multiple_of(extra + target * 256, 32)
+            total = acc[h, pl.ds(row, 256)] + dot(lhs[c, pl.ds(row, 256)], right)
+            total = total + swap(total)
+            for b in range(4):
+                upper, lower = total[64 * b : 64 * b + 32], total[64 * b + 32 : 64 * b + 64]
+                part[it, h, target * 4 + b] = jnp.where(left_lanes, upper, lower)
+            for k in range(len(PAIRS)):
+                if PAIRS[k][0] == dx:
+                    pair_copy(it, h, k).start()
 
     def update(it, h):
         here = (wide, narrow, grp)
-        remote(
-            from_pair.at[it, h], from_pair.at[it, h], p_send.at[it, h], p_recv.at[it, h], here
-        ).wait_recv()
-        total = part[it, h, narrow * 2 + grp]
-        for k in range(len(PAIRS)):
-            total = total + from_pair[it, h, k]
         far = len(FAR)
         remote(
             to_far.at[it, h, 0:far], from_far.at[it, h, 0:far], f_send.at[it, h], f_recv.at[it, h],
@@ -237,6 +244,12 @@
         high, low = halves(from_far[it, h].reshape(64, 128))
         landed = dot(place[:, 0:64], jnp.concatenate([high, low], axis=1))
         landed = landed[:, 0:128] + landed[:, 128:256]
+        remote(
+            from_pair.at[it, h], from_pair.at[it, h], p_send.at[it, h], p_recv.at[it, h], here
+        ).wait_recv()
+        total = part[it, h, narrow * 2 + grp]
+        for k in range(len(PAIRS)):
+            total = total + from_pair[it, h, k]
         one = jnp.where(left_lanes, landed[0:32], landed[96:128])
         two = jnp.where(left_lanes, landed[32:64], landed[64:96])
         residual = force[h] - (total + one + swap(two))
@@ -320,7 +333,7 @@
     both = pl.pallas_call(
         kernel,
         out_shape=jax.ShapeDtypeStruct((2, piece, 128), f32),
-        in_specs=[hbm, hbm, vmem, pl.BlockSpec(memory_space=pltpu.SMEM), vmem, vmem],
+        in_specs=[hbm, hbm, hbm, pl.BlockSpec(memory_space=pltpu.SMEM), hbm, hbm],
         out_specs=vmem,
         scratch_shapes=[
             pltpu.VMEM((slots, piece, columns), f32),
@@ -332,13 +345,16 @@
             pltpu.VMEM((ITERS, 2, pairs, piece // 2, 128), f32),
             pltpu.VMEM((ITERS, 2, blocks, 2, 128), f32),
             pltpu.VMEM((ITERS, 2, blocks, 2, 128), f32),
+            pltpu.VMEM((1, iface), jnp.int32),
+            pltpu.VMEM((1, piece), f32),
+            pltpu.VMEM((1, piece, 128), f32),
             pltpu.VMEM((blocks, 128), jnp.int32),
             pltpu.VMEM((blocks, 128), jnp.int32),
             pltpu.VMEM((2 * piece, 128), jnp.bfloat16),
             pltpu.VMEM((piece // 2, 128), f32),
             pltpu.VMEM((2, piece // 2, 128), f32),
             pltpu.VMEM((2, piece // 2, 128), f32),
-            dma((slots + 1,)),
+            dma((slots + 4,)),
             dma(()),
             dma(()),
             dma((ITERS, 2)),

time: 73.7 us -> 72.8 us (0.988)
  Pallas kernels: 70.8 us -> 69.9 us
    pallas_call x1, Pallas kernels: 70.8 us -> 69.9 us  [on_device(): pl.pallas_call(kernel, out_shape=jax.ShapeDtypeStruct((2, piece, 128), f3...]
where the time goes in v3:
time: 72.8 us; the launch traced here: 72.6 us
  Pallas kernels  69.9 us (96%)
  local copies, waits for them, and re-layouts  1.4 us (2%)
  between operations  1.29 us (2%)
    pallas_call x1, Pallas kernels, on_device(): pl.pallas_call(kernel, out_shape=jax.ShapeDtypeStruct((2, piece, 128), f3...  69.9 us

profile of v3, /device:TPU:1, one launch (start us, length us, event | category | flops | bytes accessed | tf_op | source)
XLA Modules:
  0.0 72.6 jit_solution(445351887207606715)
XLA Ops:
  1.3 69.9 %sweeps.1 = f32[2,64,128]{2,1,0:T(8,128)} custom-call(f32[16,64,1024]{2,1,0:T(8,128)} %bb.1, f32[1,48,1536]{2,1,0:T(8,128)} %schur.1, s32[1,1536]{1,0:T(1,128)} %q_hbm.1, s32[1]{0:T(128)S(6)} %copy.8.live, f32[1,64]{1,0:T(1,128)} %scale_hbm.1, f32[1,64,128]{2,1,0:T(8,128)} %exc_hbm.1), custom_call_target="tpu_custom_call" | custom-call | tf_op jit(solution)/shard_map/sweeps/pallas_call | solution.py:333
  71.2 1.4 %fusion = (f32[1,64,128]{2,1,0:T(8,128)}, f32[1,64,128]{2,1,0:T(8,128)}) fusion(f32[2,64,128]{2,1,0:T(8,128)} %sweeps.1), kind=kLoop, calls=%fused_computation | loop fusion | bytes 131072 | tf_op jit(solution)/shard_map/slice | solution.py:370

commit v4 on v3

--- a/solution.py
+++ b/solution.py
@@ -221,7 +221,6 @@
         c = len(SLOTS) // 4 - 1
         right = right_side(it, h, c)
         acc[h, 0:extra] = acc[h, 0:extra] + dot(lhs[c, 0:extra], right)
-        send_far(it, h)
         for dx in (2, 1, 3, 0):
             target = (x + dx) % NX
             row = pl.multiple_of(extra + target * 256, 32)
@@ -233,6 +232,8 @@
             for k in range(len(PAIRS)):
                 if PAIRS[k][0] == dx:
                     pair_copy(it, h, k).start()
+            if dx == 2:
+                send_far(it, h)
 
     def update(it, h):
         here = (wide, narrow, grp)
@@ -297,13 +298,15 @@
     index_tables()
     split_block(0)
     split_block(1)
+    split_block(2)
+    split_block(3)
     pl.semaphore_wait(barrier, len(FAR) + len(PAIRS) - 1)
     hand_out(0, 0)
     hand_out(0, 1)
     s_load.wait()
     s_copy = remote(sboth.at[grp], sboth.at[grp], s_send, s_recv, (wide, narrow, 1 - grp))
     s_copy.start()
-    chores = [functools.partial(split_block, 2), functools.partial(split_block, 3), s_copy.wait]
+    chores = [s_copy.wait]
     chores += [functools.partial(split_schur, c) for c in range(4)]
     for chore in chores:
         chore()

time: 72.8 us -> 73 us (level)
  no operation moved by 1% of the time
where the time goes in v4:
time: 73 us; the launch traced here: 72.8 us
  Pallas kernels  70.1 us (96%)
  local copies, waits for them, and re-layouts  1.4 us (2%)
  between operations  1.29 us (2%)
    pallas_call x1, Pallas kernels, on_device(): pl.pallas_call(kernel, out_shape=jax.ShapeDtypeStruct((2, piece, 128), f3...  70.1 us

profile of v4, /device:TPU:1, one launch (start us, length us, event | category | flops | bytes accessed | tf_op | source)
XLA Modules:
  0.0 72.8 jit_solution(12471773012433215171)
XLA Ops:
  1.3 70.1 %sweeps.1 = f32[2,64,128]{2,1,0:T(8,128)} custom-call(f32[16,64,1024]{2,1,0:T(8,128)} %bb.1, f32[1,48,1536]{2,1,0:T(8,128)} %schur.1, s32[1,1536]{1,0:T(1,128)} %q_hbm.1, s32[1]{0:T(128)S(6)} %copy.8.live, f32[1,64]{1,0:T(1,128)} %scale_hbm.1, f32[1,64,128]{2,1,0:T(8,128)} %exc_hbm.1), custom_call_target="tpu_custom_call" | custom-call | tf_op jit(solution)/shard_map/sweeps/pallas_call | solution.py:336
  71.4 1.4 %fusion = (f32[1,64,128]{2,1,0:T(8,128)}, f32[1,64,128]{2,1,0:T(8,128)}) fusion(f32[2,64,128]{2,1,0:T(8,128)} %sweeps.1), kind=kLoop, calls=%fused_computation | loop fusion | bytes 131072 | tf_op jit(solution)/shard_map/slice | solution.py:373
